TPU v7x, 256 devices: a whole 4x4x8 slice. The times are simulated.
256 devices in a mesh: cells: 64 (over x, z_lo, y), genes: 4 (over z_hi, core).
Axes of the slice: x: 4, y: 4, z: 8 (z_hi: 2, z_lo: 4; z = z_hi * 4 + z_lo), core: 2. Of those that a mesh axis runs over, the one named last changes fastest.
Arguments:
- counts: int32 [65536, 4096], P('cells', 'genes'), may hold values from 0 to 26, as said below
- library: int32 [65536], P('cells'), may hold values from 2000 to 19999
Outputs:
- adjacency: float32 [4096, 4096], P('cells', 'genes')
- connectivity: float32 [4096], P('cells')
Inputs may be any that keep to these rules, and one draw needn't show every extreme that they name: Non-negative integer counts.
All inputs are finite; a program needn't handle non-finite values.
Results may differ from a plain program's by a relative error of at most 0.006.
Values may be sent and summed in bfloat16 or wider, within the bound.
A program may use at most 128 MiB of HBM per device.

v0:
```python
import jax
import jax.numpy as jnp
from jax import lax
from jax.sharding import Mesh
from jax.sharding import PartitionSpec as P

CELLS = ("cells_0", "cells_1", "cells_2")


def from_everyone(x, axis):
    copies = jnp.broadcast_to(x, (lax.axis_size(axis), *x.shape))
    return lax.all_to_all(copies, axis, split_axis=0, concat_axis=0, tiled=True)


def of_everyone(x, axis):
    return from_everyone(x, axis).sum(axis=0)


def packed_total(arrays, axis):
    ends = [0]
    for a in arrays:
        ends.append(ends[-1] + a.size)
    total = of_everyone(jnp.concatenate([a.ravel() for a in arrays]), axis)
    return tuple((total[b:e].reshape(a.shape) for a, b, e in zip(arrays, ends, ends[1:])))


def turned_gather(arrays, axis, dims):
    turned = [jnp.moveaxis(a, dim, 0) for a, dim in zip(arrays, dims)]
    both = jnp.concatenate([t.reshape(len(t), -1) for t in turned], axis=1)
    out, at, outs = (lax.all_gather(both, axis, axis=0, tiled=True), 0, [])
    for t, dim in zip(turned, dims):
        section = out[:, at : at + t[0].size].reshape(-1, *t.shape[1:])
        outs.append(jnp.moveaxis(section, 0, dim))
        at += t[0].size
    return tuple(outs)


def sum_in_order(blocks, axes, sequence):
    inside = blocks.shape[1:]
    blocks = blocks.reshape(*(lax.axis_size(a) for a in axes), *inside)
    blocks = jnp.moveaxis(blocks, sequence, range(len(axes))).reshape(-1, *inside)
    for k in sequence:
        blocks = lax.psum_scatter(blocks, axes[k], scatter_dimension=0, tiled=True)
    return blocks[0]


def cut_along(x, dim, devices):
    dims = x.shape
    blocks = x.reshape(*dims[:dim], devices, dims[dim] // devices, *dims[dim + 1 :])
    return jnp.moveaxis(blocks, dim, 0)


def scatter_axes(x, axes, sequence, dim):
    devices = lax.axis_size(axes)
    return sum_in_order(cut_along(x, dim, devices), axes, sequence)


def normalize(counts, library):
    factor = 10000.0 / library.astype(jnp.float32)
    return jnp.log1p(counts.astype(jnp.float32) * factor[:, None]).astype(jnp.bfloat16)


def cross_product(left, right):
    return lax.dot_general(
        left, right, (((0,), (0,)), ((), ())), preferred_element_type=jnp.float32
    )


def shards(counts, library):
    own_block = normalize(counts, library)
    col_width = own_block.shape[1]
    cell_groups = lax.axis_size(CELLS)
    gene_total = col_width * lax.axis_size("genes")
    row_width = gene_total // cell_groups
    total_cells = float(counts.shape[0] * cell_groups)
    widened = own_block.astype(jnp.float32)
    local_sums = jnp.sum(widened, axis=0)
    local_squares = jnp.sum(widened * widened, axis=0)
    block_sums, block_squares = packed_total((local_sums, local_squares), CELLS)
    gene_sums, gene_squares = turned_gather((block_sums, block_squares), "genes", (0, 0))
    full_block = lax.all_gather(own_block, "genes", axis=1, tiled=True)
    gram_tile = scatter_axes(cross_product(full_block, own_block), CELLS, (0, 2, 1), 0)
    means = gene_sums / total_cells
    variances = gene_squares / total_cells - means * means
    scales = lax.rsqrt(variances + 1e-05)
    row_first = lax.axis_index(CELLS) * row_width
    col_first = lax.axis_index("genes") * col_width
    row_means = lax.dynamic_slice_in_dim(means, row_first, row_width, 0)
    col_means = lax.dynamic_slice_in_dim(means, col_first, col_width, 0)
    row_scales = lax.dynamic_slice_in_dim(scales, row_first, row_width, 0)
    col_scales = lax.dynamic_slice_in_dim(scales, col_first, col_width, 0)
    correlation = (
        (gram_tile / total_cells - row_means[:, None] * col_means[None, :])
        * row_scales[:, None]
        * col_scales[None, :]
    )
    powered = correlation**6
    row_index = row_first + jnp.arange(row_width, dtype=jnp.int32)[:, None]
    col_index = col_first + jnp.arange(col_width, dtype=jnp.int32)[None, :]
    adjacency = jnp.where(row_index == col_index, jnp.float32(0.0), powered)
    connectivity = of_everyone(jnp.sum(adjacency, axis=1), "genes")
    return (adjacency, connectivity)


def solution(mesh):
    finer = Mesh(
        mesh.devices.reshape(4, 4, 4, mesh.shape["genes"]),
        ("cells_0", "cells_1", "cells_2", "genes"),
    )
    in_specs = (P(CELLS, "genes"), P(CELLS))
    out_specs = (P(CELLS, "genes"), P(CELLS))
    return jax.shard_map(
        shards, mesh=finer, in_specs=in_specs, out_specs=out_specs, check_vma=False
    )
```

profile of v0, /device:TPU:1, one launch (start us, length us, event | category | flops | bytes accessed | tf_op | source)
XLA Modules:
  0.0 405.9 jit_solution(15591229205354031744)
XLA Ops:
  7.2 0.0 all-gather.2.cloned.1.call-start
  7.2 0.7 convert_divide_fusion
  7.9 5.6 %convert_reduce_fusion = (f32[1024]{0:T(1024)S(1)}, f32[1024]{0:T(1024)S(1)}, bf16[1024,1024]{1,0:T(8,128)(2,1)}) fusion(f32[1024]{0:T(1024)S(1)} %convert_divide_fusion, s32[1024,1024]{1,0:T(8,128)} %param.2), kind=kLoop, calls=%fused_computation.1 | loop fusion | flops 7337984 | bytes 6303744 | tf_op jit(solution)/shard_map/reduce_sum | solution.py:77
  13.5 0.0 all-gather.2.cloned.1.call-update
  13.6 0.0 reduce-scatter.4.cloned.1.call-start
  13.6 117.8 %all-gather.2.cloned.1.call-done = bf16[1024,4096]{1,0:T(8,128)(2,1)} async-done(((bf16[1024,1024]{1,0:T(8,128)(2,1)}), bf16[1024,4096]{1,0:T(8,128)(2,1)}) %all-gather.2.cloned.1.call-update) | async-done | bytes 8388624 | tf_op jit(solution)/shard_map/all_gather | solution.py:81
  131.4 12.0 %fusion.11 = f32[4096,1024]{1,0:T(8,128)S(1)} fusion(bf16[1024,4096]{1,0:T(8,128)(2,1)} %all-gather.2.cloned.1.call-done, bf16[1024,1024]{1,0:T(8,128)(2,1)} %get-tuple-element.6), kind=kOutput, calls=%fused_computation.27 | convolution fusion | flops 8589934592 | bytes 27262976 | tf_op jit(solution)/shard_map/dot_general | solution.py:64
  143.5 6.6 %copy.6 = f32[4,4,4,64,1024]{4,3,2,1,0:T(8,128)} copy(f32[4,4,4,64,1024]{4,3,1,2,0:T(8,128)S(1)} %bitcast.27) | data formatting | bytes 33554432 | tf_op jit(solution)/shard_map/transpose | solution.py:41
  150.0 0.0 reduce-scatter.4.cloned.1.call-update
  150.1 0.0 reduce-scatter.6.cloned.1.call-start
  150.1 146.2 %reduce-scatter.4.cloned.1.call-done = f32[16,64,1024]{2,1,0:T(8,128)} async-done(((f32[64,64,1024]{2,1,0:T(8,128)}), f32[16,64,1024]{2,1,0:T(8,128)}) %reduce-scatter.4.cloned.1.call-update) | async-done | bytes 4194320 | tf_op jit(solution)/shard_map/reduce_scatter | solution.py:43
  296.3 0.0 reduce-scatter.6.cloned.1.call-update
  296.4 1.1 broadcast_in_dim.8
  297.4 8.9 %all-to-all-start = ((f32[64,1,2048]{2,1,0:T(1,128)}), f32[64,1,2048]{2,1,0:T(1,128)S(1)}, u32[]{:S(2)}, u32[]{:S(2)}) async-start(f32[64,1,2048]{2,1,0:T(1,128)} %broadcast_in_dim.8), calls=%async_computation.3 | async-start | bytes 1048576 | tf_op jit(solution)/shard_map/all_to_all | solution.py:12
  306.3 0.0 reduce-scatter.8.cloned.1.call-start
  306.4 45.9 %reduce-scatter.6.cloned.1.call-done = f32[4,64,1024]{2,1,0:T(8,128)} async-done(((f32[16,64,1024]{2,1,0:T(8,128)}), f32[4,64,1024]{2,1,0:T(8,128)}) %reduce-scatter.6.cloned.1.call-update) | async-done | bytes 1048592 | tf_op jit(solution)/shard_map/reduce_scatter | solution.py:43
  352.3 0.0 reduce-scatter.8.cloned.1.call-update
  352.3 0.0 all-to-all-done
  352.3 0.3 reduce_sum.47
  352.7 9.6 %all_gather.7 = f32[4096,2]{0,1:T(2,128)S(1)} all-gather(f32[1024,2]{0,1:T(2,128)S(1)} %pad_maximum_fusion.1), channel_id=1, replica_groups=mesh['cells_0'=4,'cells_1'=4,'cells_2'=4,'genes'=4] {'genes'}, dimensions={0}, use_global_device_ids=true | all-gather | bytes 40960 | tf_op jit(solution)/shard_map/all_gather | solution.py:30
  362.3 0.1 fusion.6
  362.4 22.1 %reduce-scatter.8.cloned.1.call-done = f32[1,64,1024]{2,1,0:T(8,128)} async-done(((f32[4,64,1024]{2,1,0:T(8,128)}), f32[1,64,1024]{2,1,0:T(8,128)}) %reduce-scatter.8.cloned.1.call-update) | async-done | bytes 262160 | tf_op jit(solution)/shard_map/reduce_scatter | solution.py:43
  384.4 1.9 fusion.8
  386.4 12.4 %all_to_all.12 = f32[4,1,64]{2,1,0:T(1,128)S(1)} all-to-all(f32[4,1,64]{2,1,0:T(1,128)S(1)} %broadcast_in_dim.10), channel_id=1, replica_groups=mesh['cells_0'=4,'cells_1'=4,'cells_2'=4,'genes'=4] {'genes'}, dimensions={0} | all-to-all | bytes 2048 | tf_op jit(solution)/shard_map/all_to_all | solution.py:12
  398.8 0.5 reduce_sum.49
  (8 shorter events, 0.1 us)
Async XLA Ops:
  7.2 124.3 %all-gather.2.cloned.1.call-start = ((), (), s32[]{:S(2)}) async-start(), calls=%async_computation.5 | async-start | bytes 10485760 | tf_op jit(solution)/shard_map/all_gather | solution.py:81
  13.6 282.8 %reduce-scatter.4.cloned.1.call-start = ((), (), s32[]{:S(2)}) async-start(), calls=%async_computation.6 | async-start | bytes 20971520 | tf_op jit(solution)/shard_map/reduce_scatter | solution.py:43
  150.1 202.2 %reduce-scatter.6.cloned.1.call-start = ((), (), s32[]{:S(2)}) async-start(), calls=%async_computation.7 | async-start | bytes 5242880 | tf_op jit(solution)/shard_map/reduce_scatter | solution.py:43
  297.4 54.9 %all-to-all-start = ((f32[64,1,2048]{2,1,0:T(1,128)}), f32[64,1,2048]{2,1,0:T(1,128)S(1)}, u32[]{:S(2)}, u32[]{:S(2)}) async-start(f32[64,1,2048]{2,1,0:T(1,128)} %broadcast_in_dim.8), calls=%async_computation.3 | async-start | bytes 1048576 | tf_op jit(solution)/shard_map/all_to_all | solution.py:12
  306.3 78.1 %reduce-scatter.8.cloned.1.call-start = ((), (), s32[]{:S(2)}) async-start(), calls=%async_computation.8 | async-start | bytes 1310720 | tf_op jit(solution)/shard_map/reduce_scatter | solution.py:43
Sparse Core Ops, SparseCore 0:
  13.7 117.6 all-gather.1
  150.2 146.0 reduce-scatter.3
  298.9 53.3 reduce-scatter.5
  354.7 29.7 reduce-scatter.7
where the time goes:
time: 406 us
  waiting for transfers between devices  332 us (82%)
  blocking collectives  22 us (5%)
  between operations  13.8 us (3%)
  matrix products  12 us (3%)
  other arithmetic  9.16 us (2%)
  starting transfers between devices  9.05 us (2%)
  local copies, waits for them, and re-layouts  7.75 us (2%)
    reduce_scatter x3, waiting for transfers between devices, sum_in_order(): blocks = lax.psum_scatter(blocks, axes[k], scatter_dimension=0, tiled=True)  214 us
    all_gather x1, waiting for transfers between devices, shards(): full_block = lax.all_gather(own_block, 'genes', axis=1, tiled=True)  118 us
    all_to_all x1, blocking collectives, from_everyone(): return lax.all_to_all(copies, axis, split_axis=0, concat_axis=0, tiled=True)  12.4 us
    dot_general x1, matrix products, cross_product(): lax.dot_general(left, right, (((0,), (0,)), ((), ())), preferred_element_...  12 us
    all_gather x1, blocking collectives, turned_gather(): out, at, outs = (lax.all_gather(both, axis, axis=0, tiled=True), 0, [])  9.55 us
    all_to_all x1, starting transfers between devices, from_everyone(): return lax.all_to_all(copies, axis, split_axis=0, concat_axis=0, tiled=True)  8.89 us
  transfers between devices with their start and end apart: 5, of which 4 were waited for; matrix products, arithmetic and copies ran while one was open for 0% of the time, Pallas kernels for 0%

commit v1 on v0

--- a/solution.py
+++ b/solution.py
@@ -78,7 +78,9 @@
     local_squares = jnp.sum(widened * widened, axis=0)
     block_sums, block_squares = packed_total((local_sums, local_squares), CELLS)
     gene_sums, gene_squares = turned_gather((block_sums, block_squares), "genes", (0, 0))
-    full_block = lax.all_gather(own_block, "genes", axis=1, tiled=True)
+    full_block = jnp.concatenate(
+        lax.all_to_all(jnp.stack([own_block] * lax.axis_size("genes")), "genes", 0, 0), axis=1
+    )
     gram_tile = scatter_axes(cross_product(full_block, own_block), CELLS, (0, 2, 1), 0)
     means = gene_sums / total_cells
     variances = gene_squares / total_cells - means * means

time: 406 us -> 491 us (1.21)
  blocking collectives: 22 us -> 219 us
  waiting for transfers between devices: 332 us -> 217 us
    all_to_all x0 -> x1, blocking collectives: none -> 197 us  [shards(): lax.all_to_all(jnp.stack([own_block] * lax.axis_size('genes')), 'genes',...]
    all_gather x1 -> x0, waiting for transfers between devices: 118 us -> none  [shards(): full_block = lax.all_gather(own_block, 'genes', axis=1, tiled=True)]
  transfers between devices with their start and end apart: 5 -> 4, of which waited for: 4 -> 3; matrix products, arithmetic and copies ran while one was open for 0% -> 0% of each run, Pallas kernels for 0% -> 0%
where the time goes in v1:
time: 491 us
  blocking collectives  219 us (45%)
  waiting for transfers between devices  217 us (44%)
  between operations  13.9 us (3%)
  local copies, waits for them, and re-layouts  11.8 us (2%)
  matrix products  11.6 us (2%)
  other arithmetic  9.16 us (2%)
  starting transfers between devices  9 us (2%)
    reduce_scatter x3, waiting for transfers between devices, sum_in_order(): blocks = lax.psum_scatter(blocks, axes[k], scatter_dimension=0, tiled=True)  217 us
    all_to_all x1, blocking collectives, shards(): lax.all_to_all(jnp.stack([own_block] * lax.axis_size('genes')), 'genes',...  197 us
    all_to_all x1, blocking collectives, from_everyone(): return lax.all_to_all(copies, axis, split_axis=0, concat_axis=0, tiled=True)  12.5 us
    dot_general x1, matrix products, cross_product(): lax.dot_general(left, right, (((0,), (0,)), ((), ())), preferred_element_...  11.6 us
  transfers between devices with their start and end apart: 4, of which 3 were waited for; matrix products, arithmetic and copies ran while one was open for 0% of the time, Pallas kernels for 0%

profile of v1, /device:TPU:1, one launch (start us, length us, event | category | flops | bytes accessed | tf_op | source)
XLA Modules:
  0.0 490.8 jit_solution(13700427106023687262)
XLA Ops:
  7.2 0.0 reduce-scatter.4.cloned.1.call-start
  7.2 0.7 convert_divide_fusion
  7.9 5.6 %convert_reduce_fusion = (f32[1024]{0:T(1024)S(1)}, f32[1024]{0:T(1024)S(1)}, bf16[1024,1024]{1,0:T(8,128)(2,1)}) fusion(f32[1024]{0:T(1024)S(1)} %convert_divide_fusion, s32[1024,1024]{1,0:T(8,128)} %param.2), kind=kLoop, calls=%fused_computation.2 | loop fusion | flops 7337984 | bytes 6303744 | tf_op jit(solution)/shard_map/reduce_sum | solution.py:77
  13.5 2.9 copy.9
  16.4 1.2 stack.2
  17.6 0.0 copy-start
  17.6 196.6 %all_to_all.17 = bf16[4,1024,1024]{1,2,0:T(8,128)(2,1)} all-to-all(bf16[4,1024,1024]{1,2,0:T(8,128)(2,1)S(1)} %stack.2), channel_id=1, replica_groups=mesh['cells_0'=4,'cells_1'=4,'cells_2'=4,'genes'=4] {'genes'}, dimensions={0} | all-to-all | bytes 16777216 | tf_op jit(solution)/shard_map/all_to_all | solution.py:82
  214.2 0.0 copy-done
  214.2 11.6 %convolution_bitcast_fusion = f32[4,4,4,64,1024]{4,3,1,2,0:T(8,128)S(1)} fusion(bf16[4,4,4,64,1024]{4,3,2,1,0:T(8,128)(2,1)} %bitcast.37, bf16[1024,1024]{1,0:T(8,128)(2,1)S(1)} %copy-done), kind=kOutput, calls=%fused_computation | convolution fusion | flops 8589934592 | bytes 27262976 | tf_op jit(solution)/shard_map/dot_general | solution.py:64
  225.8 6.6 %copy.10 = f32[4,4,4,64,1024]{4,3,2,1,0:T(8,128)} copy(f32[4,4,4,64,1024]{4,3,1,2,0:T(8,128)S(1)} %convolution_bitcast_fusion) | data formatting | bytes 33554432 | tf_op jit(solution)/shard_map/transpose | solution.py:41
  232.4 0.0 reduce-scatter.4.cloned.1.call-update
  232.4 0.0 reduce-scatter.6.cloned.1.call-start
  232.4 148.6 %reduce-scatter.4.cloned.1.call-done = f32[16,64,1024]{2,1,0:T(8,128)} async-done(((f32[64,64,1024]{2,1,0:T(8,128)}), f32[16,64,1024]{2,1,0:T(8,128)}) %reduce-scatter.4.cloned.1.call-update) | async-done | bytes 4194320 | tf_op jit(solution)/shard_map/reduce_scatter | solution.py:43
  381.1 0.0 reduce-scatter.6.cloned.1.call-update
  381.1 1.1 broadcast_in_dim.8
  382.2 8.9 %all-to-all-start.1 = ((f32[64,1,2048]{2,1,0:T(1,128)}), f32[64,1,2048]{2,1,0:T(1,128)S(1)}, u32[]{:S(2)}, u32[]{:S(2)}) async-start(f32[64,1,2048]{2,1,0:T(1,128)} %broadcast_in_dim.8), calls=%async_computation.4 | async-start | bytes 1048576 | tf_op jit(solution)/shard_map/all_to_all | solution.py:12
  391.1 0.0 reduce-scatter.8.cloned.1.call-start
  391.1 45.9 %reduce-scatter.6.cloned.1.call-done = f32[4,64,1024]{2,1,0:T(8,128)} async-done(((f32[16,64,1024]{2,1,0:T(8,128)}), f32[4,64,1024]{2,1,0:T(8,128)}) %reduce-scatter.6.cloned.1.call-update) | async-done | bytes 1048592 | tf_op jit(solution)/shard_map/reduce_scatter | solution.py:43
  437.0 0.0 reduce-scatter.8.cloned.1.call-update
  437.0 0.0 all-to-all-done.1
  437.0 0.3 reduce_sum.47
  437.4 9.6 %all_gather.3 = f32[4096,2]{0,1:T(2,128)S(1)} all-gather(f32[1024,2]{0,1:T(2,128)S(1)} %pad_maximum_fusion.1), channel_id=1, replica_groups=mesh['cells_0'=4,'cells_1'=4,'cells_2'=4,'genes'=4] {'genes'}, dimensions={0}, use_global_device_ids=true | all-gather | bytes 40960 | tf_op jit(solution)/shard_map/all_gather | solution.py:30
  447.0 0.1 fusion.7
  447.1 22.2 %reduce-scatter.8.cloned.1.call-done = f32[1,64,1024]{2,1,0:T(8,128)} async-done(((f32[4,64,1024]{2,1,0:T(8,128)}), f32[1,64,1024]{2,1,0:T(8,128)}) %reduce-scatter.8.cloned.1.call-update) | async-done | bytes 262160 | tf_op jit(solution)/shard_map/reduce_scatter | solution.py:43
  469.3 1.9 fusion.9
  471.3 12.5 %all_to_all.18 = f32[4,1,64]{2,1,0:T(1,128)S(1)} all-to-all(f32[4,1,64]{2,1,0:T(1,128)S(1)} %broadcast_in_dim.10), channel_id=1, replica_groups=mesh['cells_0'=4,'cells_1'=4,'cells_2'=4,'genes'=4] {'genes'}, dimensions={0} | all-to-all | bytes 2048 | tf_op jit(solution)/shard_map/all_to_all | solution.py:12
  483.7 0.5 reduce_sum.49
  (8 shorter events, 0.1 us)
Async XLA Ops:
  7.2 373.9 %reduce-scatter.4.cloned.1.call-start = ((), (), s32[]{:S(2)}) async-start(), calls=%async_computation.6 | async-start | bytes 20971520 | tf_op jit(solution)/shard_map/reduce_scatter | solution.py:43
  17.6 196.6 %copy-start = (bf16[1024,1024]{1,0:T(8,128)(2,1)S(1)}, bf16[1024,1024]{1,0:T(8,128)(2,1)}, u32[]{:S(2)}) copy-start(bf16[1024,1024]{1,0:T(8,128)(2,1)} %get-tuple-element.6) | copy-start | bytes 6291460
  232.4 204.6 %reduce-scatter.6.cloned.1.call-start = ((), (), s32[]{:S(2)}) async-start(), calls=%async_computation.7 | async-start | bytes 5242880 | tf_op jit(solution)/shard_map/reduce_scatter | solution.py:43
  382.2 54.9 %all-to-all-start.1 = ((f32[64,1,2048]{2,1,0:T(1,128)}), f32[64,1,2048]{2,1,0:T(1,128)S(1)}, u32[]{:S(2)}, u32[]{:S(2)}) async-start(f32[64,1,2048]{2,1,0:T(1,128)} %broadcast_in_dim.8), calls=%async_computation.4 | async-start | bytes 1048576 | tf_op jit(solution)/shard_map/all_to_all | solution.py:12
  391.1 78.3 %reduce-scatter.8.cloned.1.call-start = ((), (), s32[]{:S(2)}) async-start(), calls=%async_computation.8 | async-start | bytes 1310720 | tf_op jit(solution)/shard_map/reduce_scatter | solution.py:43
Sparse Core Ops, SparseCore 0:
  232.5 148.4 reduce-scatter.3
  383.6 53.3 reduce-scatter.5
  439.5 29.7 reduce-scatter.7
